TPU v7x, 32 devices: a whole 2x2x4 slice. The times are simulated.
32 devices in a mesh: ka: 16 (over z, y, x), occ: 2 (over core).
Axes of the slice: x: 2, y: 2, z: 4, core: 2. Of those that a mesh axis runs over, the one named last changes fastest.
Arguments:
- factors: bfloat16 [32, 2, 192, 2, 768], P('ka'), may hold values from -0.23925781 to 0.23925781
- occupied_energy: float32 [2], replicated, may hold values from -2 to -0.5
- virtual_energy: bfloat16 [32, 192], P('ka'), may hold values from 0.5 to 3
- conserve: int32 [32, 2], P('ka'), may hold values from 0 to 31, as said below
- pair_lists: int32 [2, 4, 2], P(None, 'occ'), may hold values from 0 to 1, as said below
Outputs:
- density: float32 [32, 192, 2, 192], P('ka', 'occ')
Inputs may be any that keep to these rules, and one draw needn't show every extreme that they name: For a momentum ka among the 2 momenta of block d (momenta d * 2 to d * 2 + 1), (32 - conserve[ka, r]) mod 32 lies in block (d - r - 1) mod 16; the 2 momenta of one block name different momenta in each round. `pair_lists`: each entry is an ordered pair (i, j) of occupied orbitals; every round begins with the pairs (0, 0) and (1, 1); within a round no ordered pair repeats (4 of the 4 ordered pairs appear).
All inputs are finite; a program needn't handle non-finite values.
Results may differ from a plain program's by a relative error of at most 0.00082.
Values may be sent and summed in bfloat16 or wider, within the bound.
A program may use at most 128 MiB of HBM per device.

v0:
```python
import jax
import jax.numpy as jnp
from jax import lax
from jax.sharding import PartitionSpec as P


def from_behind(array, axis, by):
    size = lax.axis_size(axis)
    return lax.ppermute(array, axis, [(i, (i + by) % size) for i in range(size)])


def build_mates(received, auxiliary):
    real_part = received[..., :auxiliary]
    imaginary = received[..., auxiliary:]
    turned = jnp.concatenate([-imaginary, real_part], axis=-1)
    return jnp.concatenate([received, turned], axis=-2)


def amplitude(left_rows, mate_rows, energy_left, energy_right, occupied_sum):
    values = lax.dot_general(
        left_rows, mate_rows, (((1,), (1,)), ((), ())), preferred_element_type=jnp.float32
    )
    denominator = energy_left[:, None] + energy_right[None, :] - occupied_sum
    return values / jnp.concatenate([denominator, denominator], axis=1)


def density_term(amplitudes, swapped):
    virtuals = amplitudes.shape[0]
    combined = (2.0 * amplitudes - swapped).astype(jnp.bfloat16)
    rounded = amplitudes.astype(jnp.bfloat16)
    turned = jnp.concatenate([-rounded[:, virtuals:], rounded[:, :virtuals]], axis=1)
    stacked = jnp.concatenate([rounded, turned], axis=0)
    return lax.dot_general(
        combined, stacked, (((1,), (1,)), ((), ())), preferred_element_type=jnp.float32
    )


def pair_term(own_block, mate_block, energy_left, energy_right, occupied_energy, pair_row):
    leading = pair_row[0]
    trailing = pair_row[1]
    occupied_sum = occupied_energy[leading] + occupied_energy[trailing]
    amplitudes = amplitude(
        own_block[leading], mate_block[trailing], energy_left, energy_right, occupied_sum
    )
    swapped = amplitude(
        own_block[trailing], mate_block[leading], energy_left, energy_right, occupied_sum
    )
    return density_term(amplitudes, swapped)


def local(factors, occupied_energy, virtual_energy, conserve, pair_lists):
    momenta = factors.shape[0]
    orbitals = factors.shape[1]
    virtuals = factors.shape[2]
    auxiliary = factors.shape[4]
    own = factors.reshape(momenta, orbitals, virtuals, 2 * auxiliary)
    energy_own = virtual_energy.astype(jnp.float32)
    density = jnp.zeros((momenta, virtuals, 2 * virtuals), jnp.float32)
    for round_index in range(conserve.shape[1]):
        portion = orbitals // lax.axis_size("occ")
        portion_block = lax.dynamic_slice_in_dim(
            factors, lax.axis_index("occ") * portion, portion, 1
        )
        shifted, energy_mate = from_behind((portion_block, virtual_energy), "ka", round_index + 1)
        received = lax.all_gather(shifted, "occ", axis=1, tiled=True)
        mates = build_mates(received.reshape(momenta, orbitals, virtuals, 2 * auxiliary), auxiliary)
        energy_mate = energy_mate.astype(jnp.float32)
        for local_index in range(momenta):
            chosen = (momenta - conserve[local_index, round_index] % momenta) % momenta
            mate_block = lax.dynamic_index_in_dim(mates, chosen, 0, keepdims=False)
            energy_right = lax.dynamic_index_in_dim(energy_mate, chosen, 0, keepdims=False)
            own_block = own[local_index]
            energy_left = energy_own[local_index]

            def add_pair(partial_sum, pair_row):
                term = pair_term(
                    own_block, mate_block, energy_left, energy_right, occupied_energy, pair_row
                )
                return (partial_sum + term, None)

            running, ignored = lax.scan(add_pair, density[local_index], pair_lists[round_index])
            density = density.at[local_index].set(running)
    shaped = density.reshape(momenta, virtuals, 2, virtuals)
    return lax.psum_scatter(shaped, "occ", scatter_dimension=1, tiled=True)


def solution(mesh):
    in_specs = (
        P("ka", None, None, None, None),
        P(),
        P("ka", None),
        P("ka", None),
        P(None, "occ", None),
    )
    out_specs = P("ka", "occ", None, None)
    return jax.shard_map(local, mesh=mesh, in_specs=in_specs, out_specs=out_specs, check_vma=False)
```

profile of v0, /device:TPU:0, one launch (start us, length us, event | category | flops | bytes accessed | tf_op | source)
XLA Modules:
  0.0 199.4 jit_solution(10471028342775265886)
XLA Ops:
  6.5 3.2 %constant_dynamic-slice_fusion.8 = bf16[2,1,192,2,768]{4,3,2,1,0:T(2,128)(2,1)} fusion(bf16[2,2,192,2,768]{4,3,2,1,0:T(2,128)(2,1)} %param.21, s32[]{:T(128)S(6)} %select_n.97), kind=kLoop, calls=%fused_computation.141 | loop fusion | bytes 2359300 | tf_op jit(solution)/shard_map/dynamic_slice | solution.py:61
  9.8 3.0 %collective-permute-start = (bf16[2,1,192,2,768]{4,3,2,1,0:T(2,128)(2,1)}, bf16[2,1,192,2,768]{4,3,2,1,0:T(2,128)(2,1)S(1)}, u32[]{:S(2)}, u32[]{:S(2)}) collective-permute-start(bf16[2,1,192,2,768]{4,3,2,1,0:T(2,128)(2,1)} %constant_dynamic-slice_fusion.8), channel_id=1, source_target_pairs={{0,2},{2,4},{4,6},{6,8},{8,10},{10,12},{12,14},{14,16},{16,18},{18... | collective-permute-start | bytes 3538952 | tf_op jit(solution)/shard_map/ppermute | solution.py:9
  12.8 30.2 %collective-permute-done = bf16[2,1,192,2,768]{4,3,2,1,0:T(2,128)(2,1)S(1)} collective-permute-done((bf16[2,1,192,2,768]{4,3,2,1,0:T(2,128)(2,1)}, bf16[2,1,192,2,768]{4,3,2,1,0:T(2,128)(2,1)S(1)}, u32[]{:S(2)}, u32[]{:S(2)}) %collective-permute-start) | collective-permute-done | bytes 1179680 | tf_op jit(solution)/shard_map/ppermute | solution.py:9
  42.9 1.0 copy-done.1
  44.2 1.0 collective-permute-start.3
  45.2 0.7 fusion.169
  53.5 1.3 slice_bitcast_fusion.1
  54.8 2.7 %fusion.168 = (bf16[1,2,192,2,768]{4,3,2,1,0:T(2,128)(2,1)S(1)}, bf16[1,2,192,2,768]{4,3,2,1,0:T(2,128)(2,1)}) fusion(bf16[2,2,192,2,768]{4,3,2,1,0:T(2,128)(2,1)S(1)} %copy-done), kind=kLoop, calls=%fused_computation.156 | loop fusion | bytes 4718592 | tf_op jit(solution)/shard_map/slice | solution.py:72
  57.5 3.8 %squeeze.153 = bf16[2,192,1536]{2,1,0:T(8,128)(2,1)} reshape(bf16[1,2,192,2,768]{4,3,2,1,0:T(2,128)(2,1)} %get-tuple-element.382) | data formatting | bytes 2359296 | tf_op jit(solution)/shard_map/squeeze | solution.py:72
  61.3 1.6 squeeze.149
  62.9 8.4 %collective-permute-done.1 = bf16[2,192]{1,0:T(2,128)(2,1)} collective-permute-done((bf16[2,192]{1,0:T(2,128)(2,1)S(1)}, bf16[2,192]{1,0:T(2,128)(2,1)}, u32[]{:S(2)}, u32[]{:S(2)}) %collective-permute-start.1) | collective-permute-done | bytes 800 | tf_op jit(solution)/shard_map/ppermute | solution.py:9
  71.3 0.7 convert_element_type.34
  72.0 2.3 %collective-permute-done.3 = bf16[2,192]{1,0:T(2,128)(2,1)} collective-permute-done((bf16[2,192]{1,0:T(2,128)(2,1)S(1)}, bf16[2,192]{1,0:T(2,128)(2,1)}, u32[]{:S(2)}, u32[]{:S(2)}) %collective-permute-start.3) | collective-permute-done | bytes 800 | tf_op jit(solution)/shard_map/ppermute | solution.py:9
  74.3 0.6 convert_element_type.35
  75.2 5.4 %reshape.162 = bf16[2,2,192,1536]{3,2,1,0:T(8,128)(2,1)S(1)} reshape(bf16[2,2,192,2,768]{4,3,2,1,0:T(2,128)(2,1)} %all-gather.3.cloned.1.call-done) | data formatting | bytes 4718592 | tf_op jit(solution)/shard_map/reshape | solution.py:66
  80.8 0.4 maximum_maximum_fusion
  81.2 1.9 dynamic-slice_bitcast_fusion.3
  83.2 21.1 %while.48 = (s32[]{:T(128)}, f32[192,384]{1,0:T(8,128)S(1)}, s32[2,2]{1,0:T(2,128)S(1)}, bf16[2,192,1536]{2,1,0:T(8,128)(2,1)}, bf16[2,384,1536]{2,1,0:T(8,128)(...) while((s32[]{:T(128)}, f32[192,384]{1,0:T(8,128)S(1)}, ...), condition=%wide.region_1.2_spmd.clone, body=%wide.region_0.1_spmd.clone.sunk | while | flops 511340544 | bytes 5900063 | solution.py:81
  83.2 0.6 fusion.210
  87.4 0.6 fusion.211
  89.3 2.0 %fusion.212 = (bf16[192,384]{1,0:T(8,128)(2,1)S(1)}, f32[192,384]{1,0:T(8,128)S(1)}) fusion(f32[192,192]{1,0:T(8,128)S(1)} %add_subtract_fusion.10, bf16[2,384,1536]{2,1,0:T(8,128)(2,1)} %get-tuple-element.716, s32[]{:T(128)S(6)} %select_n.127, bf16[2,192,1536]{2,1,0:T(8,128)(2,1)} %get-tuple-element.715, s32[]{:T(128)S(6)} %select_n.126), kind=kOutput, calls=%fused_computation.152.clone.1 | convolution fusion | flops 226713600 | bytes 2359304 | tf_op jit(solution)/shard_map/while/body/eval_jaxpr/dot_general | solution.py:20
  91.4 2.3 %convolution_add_fusion.10 = f32[192,384]{1,0:T(8,128)S(1)} fusion(bf16[2,384,1536]{2,1,0:T(8,128)(2,1)} %get-tuple-element.716, s32[]{:T(128)S(6)} %select_n.126, bf16[2,192,1536]{2,1,0:T(8,128)(2,1)} %get-tuple-element.715, s32[]{:T(128)S(6)} %select_n.127, bf16[192,192]{1,0:T(8,128)(2,1)S(1)} %get-tuple-element.638, ...), kind=kOutput, calls=%fused_computation.70.clone.1 | convolution fusion | flops 284516352 | bytes 3096585 | tf_op jit(solution)/shard_map/while/body/eval_jaxpr/dot_general | solution.py:33
  93.8 0.6 fusion.210
  97.9 0.6 fusion.211
  99.8 2.0 %fusion.212 = (bf16[192,384]{1,0:T(8,128)(2,1)S(1)}, f32[192,384]{1,0:T(8,128)S(1)}) fusion(f32[192,192]{1,0:T(8,128)S(1)} %add_subtract_fusion.10, bf16[2,384,1536]{2,1,0:T(8,128)(2,1)} %get-tuple-element.716, s32[]{:T(128)S(6)} %select_n.127, bf16[2,192,1536]{2,1,0:T(8,128)(2,1)} %get-tuple-element.715, s32[]{:T(128)S(6)} %select_n.126), kind=kOutput, calls=%fused_computation.152.clone.1 | convolution fusion | flops 226713600 | bytes 2359304 | tf_op jit(solution)/shard_map/while/body/eval_jaxpr/dot_general | solution.py:20
  102.0 2.3 %convolution_add_fusion.10 = f32[192,384]{1,0:T(8,128)S(1)} fusion(bf16[2,384,1536]{2,1,0:T(8,128)(2,1)} %get-tuple-element.716, s32[]{:T(128)S(6)} %select_n.126, bf16[2,192,1536]{2,1,0:T(8,128)(2,1)} %get-tuple-element.715, s32[]{:T(128)S(6)} %select_n.127, bf16[192,192]{1,0:T(8,128)(2,1)S(1)} %get-tuple-element.638, ...), kind=kOutput, calls=%fused_computation.70.clone.1 | convolution fusion | flops 284516352 | bytes 3096585 | tf_op jit(solution)/shard_map/while/body/eval_jaxpr/dot_general | solution.py:33
  104.3 23.1 %while.49 = (s32[]{:T(128)}, f32[192,384]{1,0:T(8,128)}, s32[2,2]{1,0:T(2,128)S(1)}, bf16[2,192,1536]{2,1,0:T(8,128)(2,1)}, bf16[2,384,1536]{2,1,0:T(8,128)(2,1)...) while((s32[]{:T(128)}, f32[192,384]{1,0:T(8,128)}, ...), condition=%wide.region_3.4_spmd.clone, body=%wide.region_2.3_spmd.clone.sunk | while | flops 511340544 | bytes 6047519 | solution.py:81
  104.4 0.6 fusion.216
  108.7 0.6 fusion.217
  110.7 2.4 %fusion.218 = (bf16[192,384]{1,0:T(8,128)(2,1)S(1)}, f32[192,384]{1,0:T(8,128)}) fusion(f32[192,192]{1,0:T(8,128)S(1)} %add_subtract_fusion.11, bf16[2,384,1536]{2,1,0:T(8,128)(2,1)S(1)} %get-tuple-element.683, s32[]{:T(128)S(6)} %select_n.129, bf16[2,192,1536]{2,1,0:T(8,128)(2,1)} %get-tuple-element.682, s32[]{:T(128)S(6)} %select_n.128), kind=kOutput, calls=%fused_computation.155.clone.1 | convolution fusion | flops 226713600 | bytes 2408456 | tf_op jit(solution)/shard_map/while/body/eval_jaxpr/dot_general | solution.py:20
  113.2 2.7 %convolution_add_fusion.11 = f32[192,384]{1,0:T(8,128)} fusion(bf16[2,384,1536]{2,1,0:T(8,128)(2,1)S(1)} %get-tuple-element.683, s32[]{:T(128)S(6)} %select_n.128, bf16[2,192,1536]{2,1,0:T(8,128)(2,1)} %get-tuple-element.682, s32[]{:T(128)S(6)} %select_n.129, bf16[192,192]{1,0:T(8,128)(2,1)S(1)} %get-tuple-element.654, ...), kind=kOutput, calls=%fused_computation.101.clone.1 | convolution fusion | flops 284516352 | bytes 3194889 | tf_op jit(solution)/shard_map/while/body/eval_jaxpr/dot_general | solution.py:33
  115.8 0.6 fusion.216
  120.2 0.6 fusion.217
  122.2 2.4 %fusion.218 = (bf16[192,384]{1,0:T(8,128)(2,1)S(1)}, f32[192,384]{1,0:T(8,128)}) fusion(f32[192,192]{1,0:T(8,128)S(1)} %add_subtract_fusion.11, bf16[2,384,1536]{2,1,0:T(8,128)(2,1)S(1)} %get-tuple-element.683, s32[]{:T(128)S(6)} %select_n.129, bf16[2,192,1536]{2,1,0:T(8,128)(2,1)} %get-tuple-element.682, s32[]{:T(128)S(6)} %select_n.128), kind=kOutput, calls=%fused_computation.155.clone.1 | convolution fusion | flops 226713600 | bytes 2408456 | tf_op jit(solution)/shard_map/while/body/eval_jaxpr/dot_general | solution.py:20
  124.6 2.8 %convolution_add_fusion.11 = f32[192,384]{1,0:T(8,128)} fusion(bf16[2,384,1536]{2,1,0:T(8,128)(2,1)S(1)} %get-tuple-element.683, s32[]{:T(128)S(6)} %select_n.128, bf16[2,192,1536]{2,1,0:T(8,128)(2,1)} %get-tuple-element.682, s32[]{:T(128)S(6)} %select_n.129, bf16[192,192]{1,0:T(8,128)(2,1)S(1)} %get-tuple-element.654, ...), kind=kOutput, calls=%fused_computation.101.clone.1 | convolution fusion | flops 284516352 | bytes 3194889 | tf_op jit(solution)/shard_map/while/body/eval_jaxpr/dot_general | solution.py:33
  127.4 5.3 %reshape.164 = bf16[2,2,192,1536]{3,2,1,0:T(8,128)(2,1)S(1)} reshape(bf16[2,2,192,2,768]{4,3,2,1,0:T(2,128)(2,1)} %all-gather.5.cloned.1.call-done) | data formatting | bytes 4718592 | tf_op jit(solution)/shard_map/reshape | solution.py:66
  132.9 0.4 maximum_maximum_fusion.1
  133.3 1.9 dynamic-slice_bitcast_fusion
  135.2 22.5 %while.46 = (s32[]{:T(128)}, f32[192,384]{1,0:T(8,128)S(1)}, s32[2,2]{1,0:T(2,128)S(1)}, bf16[2,192,1536]{2,1,0:T(8,128)(2,1)}, bf16[2,384,1536]{2,1,0:T(8,128)(...) while((s32[]{:T(128)}, f32[192,384]{1,0:T(8,128)S(1)}, ...), condition=%wide.region_5.6_spmd, body=%wide.region_4.5_spmd.sunk | while | flops 511266816 | bytes 5900053 | solution.py:81
  135.2 0.6 fusion.198
  139.3 0.6 fusion.199
  141.3 2.7 %fusion.200 = (bf16[192,384]{1,0:T(8,128)(2,1)S(1)}, f32[192,384]{1,0:T(8,128)}) fusion(f32[192,192]{1,0:T(8,128)S(1)} %add_subtract_fusion.8, bf16[2,384,1536]{2,1,0:T(8,128)(2,1)} %get-tuple-element.749, s32[]{:T(128)S(6)} %select_n.123, bf16[2,192,1536]{2,1,0:T(8,128)(2,1)} %get-tuple-element.748, s32[]{:T(128)S(6)} %select_n.122), kind=kOutput, calls=%fused_computation.146.clone.1 | convolution fusion | flops 226713600 | bytes 2359304 | tf_op jit(solution)/shard_map/while/body/eval_jaxpr/dot_general | solution.py:20
  144.1 2.3 %convolution_add_fusion.8 = f32[192,384]{1,0:T(8,128)S(1)} fusion(f32[192,384]{1,0:T(8,128)S(1)} %get-tuple-element.735, bf16[2,384,1536]{2,1,0:T(8,128)(2,1)} %get-tuple-element.749, s32[]{:T(128)S(6)} %select_n.122, bf16[2,192,1536]{2,1,0:T(8,128)(2,1)} %get-tuple-element.748, s32[]{:T(128)S(6)} %select_n.123, ...), kind=kOutput, calls=%fused_computation.8.clone.1 | convolution fusion | flops 284442624 | bytes 3096584 | tf_op jit(solution)/shard_map/while/body/eval_jaxpr/dot_general | solution.py:33
  146.4 0.6 fusion.198
  150.6 0.6 fusion.199
  152.5 2.7 %fusion.200 = (bf16[192,384]{1,0:T(8,128)(2,1)S(1)}, f32[192,384]{1,0:T(8,128)}) fusion(f32[192,192]{1,0:T(8,128)S(1)} %add_subtract_fusion.8, bf16[2,384,1536]{2,1,0:T(8,128)(2,1)} %get-tuple-element.749, s32[]{:T(128)S(6)} %select_n.123, bf16[2,192,1536]{2,1,0:T(8,128)(2,1)} %get-tuple-element.748, s32[]{:T(128)S(6)} %select_n.122), kind=kOutput, calls=%fused_computation.146.clone.1 | convolution fusion | flops 226713600 | bytes 2359304 | tf_op jit(solution)/shard_map/while/body/eval_jaxpr/dot_general | solution.py:20
  155.3 2.3 %convolution_add_fusion.8 = f32[192,384]{1,0:T(8,128)S(1)} fusion(f32[192,384]{1,0:T(8,128)S(1)} %get-tuple-element.735, bf16[2,384,1536]{2,1,0:T(8,128)(2,1)} %get-tuple-element.749, s32[]{:T(128)S(6)} %select_n.122, bf16[2,192,1536]{2,1,0:T(8,128)(2,1)} %get-tuple-element.748, s32[]{:T(128)S(6)} %select_n.123, ...), kind=kOutput, calls=%fused_computation.8.clone.1 | convolution fusion | flops 284442624 | bytes 3096584 | tf_op jit(solution)/shard_map/while/body/eval_jaxpr/dot_general | solution.py:33
  157.7 1.0 pad_maximum_fusion.8
  158.7 0.7 slice_bitcast_fusion
  159.5 23.7 %while.47 = (s32[]{:T(128)}, f32[192,384]{1,0:T(8,128)}, s32[2,2]{1,0:T(2,128)S(1)}, bf16[2,192,1536]{2,1,0:T(8,128)(2,1)}, bf16[2,384,1536]{2,1,0:T(8,128)(2,1)...) while((s32[]{:T(128)}, f32[192,384]{1,0:T(8,128)}, ...), condition=%wide.region_7.8_spmd, body=%wide.region_6.7_spmd.sunk | while | flops 511266816 | bytes 6047509 | solution.py:81
  159.5 0.7 fusion.204
  164.0 0.7 fusion.205
  166.1 2.4 %fusion.206 = (bf16[192,384]{1,0:T(8,128)(2,1)S(1)}, f32[192,384]{1,0:T(8,128)}) fusion(f32[192,192]{1,0:T(8,128)S(1)} %add_subtract_fusion.9, bf16[2,384,1536]{2,1,0:T(8,128)(2,1)S(1)} %get-tuple-element.782, s32[]{:T(128)S(6)} %select_n.125, bf16[2,192,1536]{2,1,0:T(8,128)(2,1)} %get-tuple-element.781, s32[]{:T(128)S(6)} %select_n.124), kind=kOutput, calls=%fused_computation.149.clone.1 | convolution fusion | flops 226713600 | bytes 2408456 | tf_op jit(solution)/shard_map/while/body/eval_jaxpr/dot_general | solution.py:20
  168.6 2.8 %convolution_add_fusion.9 = f32[192,384]{1,0:T(8,128)} fusion(f32[192,384]{1,0:T(8,128)} %get-tuple-element.768, bf16[2,384,1536]{2,1,0:T(8,128)(2,1)S(1)} %get-tuple-element.782, s32[]{:T(128)S(6)} %select_n.124, bf16[2,192,1536]{2,1,0:T(8,128)(2,1)} %get-tuple-element.781, s32[]{:T(128)S(6)} %select_n.125, ...), kind=kOutput, calls=%fused_computation.39.clone.1 | convolution fusion | flops 284442624 | bytes 3194888 | tf_op jit(solution)/shard_map/while/body/eval_jaxpr/dot_general | solution.py:33
  171.3 0.7 fusion.204
  175.9 0.7 fusion.205
  178.0 2.4 %fusion.206 = (bf16[192,384]{1,0:T(8,128)(2,1)S(1)}, f32[192,384]{1,0:T(8,128)}) fusion(f32[192,192]{1,0:T(8,128)S(1)} %add_subtract_fusion.9, bf16[2,384,1536]{2,1,0:T(8,128)(2,1)S(1)} %get-tuple-element.782, s32[]{:T(128)S(6)} %select_n.125, bf16[2,192,1536]{2,1,0:T(8,128)(2,1)} %get-tuple-element.781, s32[]{:T(128)S(6)} %select_n.124), kind=kOutput, calls=%fused_computation.149.clone.1 | convolution fusion | flops 226713600 | bytes 2408456 | tf_op jit(solution)/shard_map/while/body/eval_jaxpr/dot_general | solution.py:20
  180.4 2.8 %convolution_add_fusion.9 = f32[192,384]{1,0:T(8,128)} fusion(f32[192,384]{1,0:T(8,128)} %get-tuple-element.768, bf16[2,384,1536]{2,1,0:T(8,128)(2,1)S(1)} %get-tuple-element.782, s32[]{:T(128)S(6)} %select_n.124, bf16[2,192,1536]{2,1,0:T(8,128)(2,1)} %get-tuple-element.781, s32[]{:T(128)S(6)} %select_n.125, ...), kind=kOutput, calls=%fused_computation.39.clone.1 | convolution fusion | flops 284442624 | bytes 3194888 | tf_op jit(solution)/shard_map/while/body/eval_jaxpr/dot_general | solution.py:33
  183.2 1.0 bitcast_dynamic-update-slice_fusion
  184.2 0.6 reshape.167
  185.0 1.6 reshape.168
  186.6 4.0 %reduce-scatter.4.cloned.1.call-done = f32[96,768]{1,0:T(8,128)} async-done(((f32[192,768]{1,0:T(8,128)}), f32[96,768]{1,0:T(8,128)}) %reduce-scatter.4.cloned.1.call-update) | async-done | bytes 294928
  190.6 1.3 reshape.169
  192.0 0.9 copy.7
  (62 shorter events, 2.7 us)
Async XLA Ops:
  6.5 48.3 %copy-start = (bf16[2,2,192,2,768]{4,3,2,1,0:T(2,128)(2,1)S(1)}, bf16[2,2,192,2,768]{4,3,2,1,0:T(2,128)(2,1)}, u32[]{:S(2)}) copy-start(bf16[2,2,192,2,768]{4,3,2,1,0:T(2,128)(2,1)} %param.21) | copy-start | bytes 7077892
  6.5 37.5 %copy-start.5 = (bf16[2,192]{1,0:T(2,128)(2,1)S(1)}, bf16[2,192]{1,0:T(2,128)(2,1)}, u32[]{:S(2)}) copy-start(bf16[2,192]{1,0:T(2,128)(2,1)} %param.23) | copy-start | bytes 2308
  6.5 38.6 %copy-start.4 = (s32[2,2]{1,0:T(2,128)S(1)}, s32[2,2]{1,0:T(2,128)}, u32[]{:S(2)}) copy-start(s32[2,2]{1,0:T(2,128)} %param.24) | copy-start | bytes 52
  6.5 68.7 %all-gather.3.cloned.1.call-start = ((), (), s32[]{:S(2)}) async-start(), calls=%async_computation.1 | async-start | bytes 3538944 | tf_op jit(solution)/shard_map/all_gather | solution.py:65
  9.8 33.1 %collective-permute-start = (bf16[2,1,192,2,768]{4,3,2,1,0:T(2,128)(2,1)}, bf16[2,1,192,2,768]{4,3,2,1,0:T(2,128)(2,1)S(1)}, u32[]{:S(2)}, u32[]{:S(2)}) collective-permute-start(bf16[2,1,192,2,768]{4,3,2,1,0:T(2,128)(2,1)} %constant_dynamic-slice_fusion.8), channel_id=1, source_target_pairs={{0,2},{2,4},{4,6},{6,8},{8,10},{10,12},{12,14},{14,16},{16,18},{18... | collective-permute-start | bytes 3538952 | tf_op jit(solution)/shard_map/ppermute | solution.py:9
  42.9 1.0 copy-start.1
  44.0 83.4 %all-gather.5.cloned.1.call-start = ((), (), s32[]{:S(2)}) async-start(), calls=%async_computation.2 | async-start | bytes 3538944 | tf_op jit(solution)/shard_map/all_gather | solution.py:65
  44.0 30.9 %collective-permute-start.2 = (bf16[2,1,192,2,768]{4,3,2,1,0:T(2,128)(2,1)}, bf16[2,1,192,2,768]{4,3,2,1,0:T(2,128)(2,1)}, u32[]{:S(2)}, u32[]{:S(2)}) collective-permute-start(bf16[2,1,192,2,768]{4,3,2,1,0:T(2,128)(2,1)} %constant_dynamic-slice_fusion.8), channel_id=1, source_target_pairs={{0,4},{2,6},{4,8},{6,10},{8,12},{10,14},{12,16},{14,18},{16,20},{1... | collective-permute-start | bytes 3538952 | tf_op jit(solution)/shard_map/ppermute | solution.py:9
  44.1 27.2 %collective-permute-start.1 = (bf16[2,192]{1,0:T(2,128)(2,1)S(1)}, bf16[2,192]{1,0:T(2,128)(2,1)}, u32[]{:S(2)}, u32[]{:S(2)}) collective-permute-start(bf16[2,192]{1,0:T(2,128)(2,1)S(1)} %copy-done.5), channel_id=1, source_target_pairs={{0,2},{2,4},{4,6},{6,8},{8,10},{10,12},{12,14},{14,16},{16,18},{18... | collective-permute-start | bytes 2312 | tf_op jit(solution)/shard_map/ppermute | solution.py:9
  44.2 30.1 %collective-permute-start.3 = (bf16[2,192]{1,0:T(2,128)(2,1)S(1)}, bf16[2,192]{1,0:T(2,128)(2,1)}, u32[]{:S(2)}, u32[]{:S(2)}) collective-permute-start(bf16[2,192]{1,0:T(2,128)(2,1)S(1)} %copy-done.5), channel_id=1, source_target_pairs={{0,4},{2,6},{4,8},{6,10},{8,12},{10,14},{12,16},{14,18},{16,20},{1... | collective-permute-start | bytes 2312 | tf_op jit(solution)/shard_map/ppermute | solution.py:9
  75.0 115.7 %reduce-scatter.4.cloned.1.call-start = ((), (), s32[]{:S(2)}) async-start(), calls=%async_computation.3 | async-start | bytes 884736
  81.2 2.0 copy-start.2
  81.2 1.9 copy-start.3
  81.2 1.9 copy-start.8
  133.3 1.9 copy-start.6
  157.7 1.8 copy-start.7
Sparse Core Ops, SparseCore 0:
  44.1 8.4 all-gather.2
  75.1 6.8 all-gather.4
  186.8 3.8 reduce-scatter.3
where the time goes:
time: 201 us; the launch traced here: 199 us
  local copies, waits for them, and re-layouts  45.3 us (23%)
  waiting for transfers between devices  45 us (22%)
  loops' own time  39.8 us (20%)
  matrix products  39.1 us (19%)
  between operations  21 us (10%)
  other arithmetic  4.87 us (2%)
  starting transfers between devices  4.36 us (2%)
    ppermute x4, waiting for transfers between devices, from_behind(): lax.ppermute(array, axis, [(i, (i + by) % size) for i in range(size)])  40.9 us
    another operation x4, loops' own time, local(): lax.scan(add_pair, density[local_index], pair_lists[round_index])  39.8 us
    dot_general x8, matrix products, density_term(): lax.dot_general(combined, stacked, (((1,), (1,)), ((), ())), preferred_el...  20.2 us
    dot_general x8, matrix products, amplitude(): lax.dot_general(left_rows, mate_rows, (((1,), (1,)), ((), ())), preferred...  18.9 us
    reshape x2, local copies, waits for them, and re-layouts, local(): received.reshape(momenta, orbitals, virtuals, 2 * auxiliary)  10.7 us
    squeeze x2, local copies, waits for them, and re-layouts, local(): own_block = own[local_index]  5.41 us
    unnamed x23, local copies, waits for them, and re-layouts  5.14 us
    dynamic_slice x8, local copies, waits for them, and re-layouts, pair_term(): occupied_sum = occupied_energy[leading] + occupied_energy[trailing]  5.05 us
  transfers between devices with their start and end apart: 7, of which 4 were waited for; matrix products, arithmetic and copies ran while one was open for 22% of the time, Pallas kernels for 0%

commit v1 on v0

--- a/solution.py
+++ b/solution.py
@@ -1,7 +1,15 @@
+import functools
+
 import jax
 import jax.numpy as jnp
 from jax import lax
+from jax.experimental import pallas as pl
+from jax.experimental.pallas import tpu as pltpu
 from jax.sharding import PartitionSpec as P
+
+LANES = 128
+BAND = 64
+PIECE = 16
 
 
 def from_behind(array, axis, by):
@@ -48,7 +56,7 @@
     return density_term(amplitudes, swapped)
 
 
-def local(factors, occupied_energy, virtual_energy, conserve, pair_lists):
+def general(factors, occupied_energy, virtual_energy, conserve, pair_lists):
     momenta = factors.shape[0]
     orbitals = factors.shape[1]
     virtuals = factors.shape[2]
@@ -84,6 +92,267 @@
     return lax.psum_scatter(shaped, "occ", scatter_dimension=1, tiled=True)
 
 
+def fused_kernel(
+    ring, virtuals, strips,
+    conserve_ref, occupied_ref, energy_ref, factors_ref, out_ref,
+    own_raw, mate_raw, wide, own, mate, energy_in, energy_left, energy_rows, products, total, incoming,
+    own_sem, far_send, far_recv, near_send, near_recv,
+    energy_send, energy_recv, swap_send, swap_recv,
+):
+    mesh_id = pl.DeviceIdType.MESH
+    me = lax.axis_index("ka")
+    core = lax.axis_index("occ")
+    other = 1 - core
+    odd = lax.rem(me, 2)
+    span = 2 * strips
+    half = virtuals // 2
+    pieces = virtuals // PIECE
+    bands = virtuals // BAND
+    subs = BAND // PIECE
+
+    def at(step):
+        return lax.rem(me + step + ring, ring)
+
+    near = at(1 - 2 * odd)
+
+    own_copy = pltpu.make_async_copy(factors_ref, own_raw, own_sem)
+    own_copy.start()
+
+    barrier = pltpu.get_barrier_semaphore()
+    for step in (1, 2, -1, -2):
+        pl.semaphore_signal(barrier, inc=1, device_id=(at(step), core), device_id_type=mesh_id)
+    pl.semaphore_signal(barrier, inc=1, device_id=(me, other), device_id_type=mesh_id)
+    pl.semaphore_wait(barrier, 5)
+
+    def rows_of(piece):
+        return pl.ds(pl.multiple_of(piece * (PIECE * span), PIECE * span), PIECE * span)
+
+    def far_copy(piece):
+        return pltpu.make_async_remote_copy(
+            src_ref=factors_ref.at[core, :, rows_of(piece), :],
+            dst_ref=mate_raw.at[1, :, rows_of(piece), :],
+            send_sem=far_send.at[piece], recv_sem=far_recv.at[piece],
+            device_id=(at(2), core), device_id_type=mesh_id,
+        )
+
+    def near_copy(piece, relay):
+        source = mate_raw.at[1] if relay else factors_ref.at[core]
+        return pltpu.make_async_remote_copy(
+            src_ref=source.at[:, rows_of(piece), :],
+            dst_ref=mate_raw.at[0, :, rows_of(piece), :],
+            send_sem=near_send.at[piece], recv_sem=near_recv.at[piece],
+            device_id=(near, core), device_id_type=mesh_id,
+        )
+
+    def energy_copy(slot):
+        return pltpu.make_async_remote_copy(
+            src_ref=energy_ref, dst_ref=energy_in.at[slot],
+            send_sem=energy_send.at[slot], recv_sem=energy_recv.at[slot],
+            device_id=(at(slot + 1), core), device_id_type=mesh_id,
+        )
+
+    energy_copy(0).start()
+    energy_copy(1).start()
+
+    def send_piece(piece, carry):
+        far_copy(piece).start()
+
+        @pl.when(odd == 0)
+        def _():
+            near_copy(piece, False).start()
+
+        return carry
+
+    lax.fori_loop(0, pieces, send_piece, 0)
+
+    chosen = []
+    for slot in range(2):
+        mirror = lax.rem(2 - lax.rem(conserve_ref[0, slot], 2), 2)
+        chosen.append(jnp.where(mirror == core, 0, 1))
+
+    total[...] = jnp.zeros_like(total)
+    own_copy.wait()
+
+    def shape_own(step, carry):
+        momentum_orbital = step // pieces
+        piece = lax.rem(step, pieces)
+        momentum = momentum_orbital // 2
+        orbital = lax.rem(momentum_orbital, 2)
+        wide[...] = own_raw[momentum, orbital, rows_of(piece), :].astype(jnp.float32)
+        row = pl.ds(pl.multiple_of(orbital * virtuals + piece * PIECE, PIECE), PIECE)
+        for column in range(span):
+            block = wide[pl.ds(column, PIECE, stride=span), :].astype(jnp.bfloat16)
+            own[momentum, row, pl.ds(column * LANES, LANES)] = block
+        return carry
+
+    lax.fori_loop(0, 4 * pieces, shape_own, 0)
+
+    diagonal = lax.broadcasted_iota(jnp.int32, (virtuals, virtuals), 0) == lax.broadcasted_iota(
+        jnp.int32, (virtuals, virtuals), 1
+    )
+    mine = energy_ref[...].astype(jnp.float32)
+    for momentum in range(2):
+        spread = jnp.where(diagonal, mine[momentum : momentum + 1, :], 0.0)
+        column = jnp.sum(spread, axis=1, keepdims=True)
+        energy_left[momentum] = jnp.broadcast_to(column, (virtuals, LANES))
+    for slot in range(2):
+        energy_copy(slot).wait()
+        theirs = energy_in[slot].astype(jnp.float32)
+        theirs = jnp.where(core == 0, theirs[0:1, :], theirs[1:2, :])
+        for band in range(bands):
+            part = theirs[:, band * BAND : (band + 1) * BAND]
+            energy_rows[slot, band] = jnp.broadcast_to(
+                jnp.concatenate([part, part], axis=1), (8, LANES)
+            )
+
+    sign = jnp.where(lax.broadcasted_iota(jnp.int32, (virtuals, LANES), 1) < BAND, -1.0, 1.0)
+
+    def shape_mate(slot, piece, sub):
+        for orbital in range(2):
+            wide[...] = mate_raw[slot, orbital, rows_of(piece), :].astype(jnp.float32)
+            first = orbital * 2 * BAND + sub * PIECE
+            plain = pl.ds(pl.multiple_of(first, PIECE), PIECE)
+            turned = pl.ds(pl.multiple_of(first + BAND, PIECE), PIECE)
+            for strip in range(strips):
+                real = wide[pl.ds(2 * strip, PIECE, stride=span), :]
+                imaginary = wide[pl.ds(2 * strip + 1, PIECE, stride=span), :]
+                left = pl.ds(2 * strip * LANES, LANES)
+                right = pl.ds((2 * strip + 1) * LANES, LANES)
+                mate[slot, plain, left] = real.astype(jnp.bfloat16)
+                mate[slot, plain, right] = imaginary.astype(jnp.bfloat16)
+                mate[slot, turned, left] = (-imaginary).astype(jnp.bfloat16)
+                mate[slot, turned, right] = real.astype(jnp.bfloat16)
+
+    def add_band(slot, band):
+        momentum = chosen[slot]
+        products[...] = lax.dot_general(
+            own[momentum], mate[slot], (((1,), (1,)), ((), ())), preferred_element_type=jnp.float32
+        )
+        base = energy_left[momentum] + energy_rows[slot, band][0:1, :]
+        amplitudes = {}
+        for i in range(2):
+            for j in range(2):
+                gap = base - (occupied_ref[i] + occupied_ref[j])
+                value = products[i * virtuals : (i + 1) * virtuals, j * LANES : (j + 1) * LANES]
+                amplitudes[i, j] = value / gap
+        combined, rounded, turned = [], [], []
+        for i in range(2):
+            for j in range(2):
+                this = amplitudes[i, j]
+                combined.append((2.0 * this - amplitudes[j, i]).astype(jnp.bfloat16))
+                rounded.append(this.astype(jnp.bfloat16))
+                turned.append((pltpu.roll(this, BAND, 1) * sign).astype(jnp.bfloat16))
+        left = jnp.concatenate(combined, axis=1)
+        right = jnp.concatenate(
+            [jnp.concatenate(rounded, axis=1), jnp.concatenate(turned, axis=1)], axis=0
+        )
+        total[slot] += lax.dot_general(
+            left, right, (((1,), (1,)), ((), ())), preferred_element_type=jnp.float32
+        )
+
+    def band_step(band, carry):
+        def piece_step(sub, inner):
+            piece = band * subs + sub
+            far_copy(piece).wait_recv()
+
+            @pl.when(odd == 1)
+            def _():
+                near_copy(piece, True).start()
+
+            shape_mate(1, piece, sub)
+            near_copy(piece, False).wait_recv()
+            shape_mate(0, piece, sub)
+            return inner
+
+        lax.fori_loop(0, subs, piece_step, 0)
+        add_band(1, band)
+        add_band(0, band)
+        return carry
+
+    lax.fori_loop(0, bands, band_step, 0)
+
+    def swap_copy(slot):
+        return pltpu.make_async_remote_copy(
+            src_ref=total.at[slot, pl.ds(pl.multiple_of(other * half, half), half), :],
+            dst_ref=incoming.at[slot],
+            send_sem=swap_send.at[slot], recv_sem=swap_recv.at[slot],
+            device_id=(me, other), device_id_type=mesh_id,
+        )
+
+    for slot in (1, 0):
+        swap_copy(slot).start()
+    for slot in (1, 0):
+        swap_copy(slot).wait()
+
+    here = pl.ds(pl.multiple_of(core * half, half), half)
+    for momentum in range(2):
+        value = jnp.zeros((half, 2 * virtuals), jnp.float32)
+        for slot in (1, 0):
+            value += jnp.where(chosen[slot] == momentum, total[slot, here, :], incoming[slot])
+        for part in range(2):
+            out_ref[momentum, :, part, :] = value[:, part * virtuals : (part + 1) * virtuals]
+
+    def drain(piece, carry):
+        far_copy(piece).wait_send()
+        near_copy(piece, False).wait_send()
+        return carry
+
+    lax.fori_loop(0, pieces, drain, 0)
+
+
+def fused(factors, occupied_energy, virtual_energy, conserve, pair_lists):
+    momenta, orbitals, virtuals, parts, auxiliary = factors.shape
+    strips = auxiliary // LANES
+    ring = lax.axis_size("ka")
+    raw_rows = virtuals * parts * strips
+    raw = factors.reshape(momenta, orbitals, virtuals, parts, strips, LANES)
+    raw = raw.transpose(0, 1, 2, 4, 3, 5).reshape(momenta, orbitals, raw_rows, LANES)
+    pieces = virtuals // PIECE
+    dma = pltpu.SemaphoreType.DMA
+    return pl.pallas_call(
+        functools.partial(fused_kernel, ring, virtuals, strips),
+        out_shape=jax.ShapeDtypeStruct((momenta, virtuals // 2, 2, virtuals), jnp.float32),
+        in_specs=[
+            pl.BlockSpec(memory_space=pltpu.SMEM),
+            pl.BlockSpec(memory_space=pltpu.SMEM),
+            pl.BlockSpec(memory_space=pltpu.VMEM),
+            pl.BlockSpec(memory_space=pl.ANY),
+        ],
+        out_specs=pl.BlockSpec(memory_space=pltpu.VMEM),
+        scratch_shapes=[
+            pltpu.VMEM((momenta, orbitals, raw_rows, LANES), jnp.bfloat16),
+            pltpu.VMEM((2, orbitals, raw_rows, LANES), jnp.bfloat16),
+            pltpu.VMEM((PIECE * parts * strips, LANES), jnp.float32),
+            pltpu.VMEM((momenta, orbitals * virtuals, parts * auxiliary), jnp.bfloat16),
+            pltpu.VMEM((2, orbitals * 2 * BAND, parts * auxiliary), jnp.bfloat16),
+            pltpu.VMEM((2, momenta, virtuals), jnp.bfloat16),
+            pltpu.VMEM((momenta, virtuals, LANES), jnp.float32),
+            pltpu.VMEM((2, virtuals // BAND, 8, LANES), jnp.float32),
+            pltpu.VMEM((orbitals * virtuals, orbitals * 2 * BAND), jnp.float32),
+            pltpu.VMEM((2, virtuals, 2 * virtuals), jnp.float32),
+            pltpu.VMEM((2, virtuals // 2, 2 * virtuals), jnp.float32),
+            dma,
+            dma((pieces,)), dma((pieces,)), dma((pieces,)), dma((pieces,)),
+            dma((2,)), dma((2,)), dma((2,)), dma((2,)),
+        ],
+        compiler_params=pltpu.CompilerParams(
+            collective_id=0, has_side_effects=True, vmem_limit_bytes=48 * 1024 * 1024
+        ),
+        name="density",
+    )(conserve, occupied_energy, virtual_energy, raw)
+
+
+def local(factors, occupied_energy, virtual_energy, conserve, pair_lists):
+    momenta, orbitals, virtuals, parts, auxiliary = factors.shape
+    rounds, pairs = pair_lists.shape[:2]
+    ring, holders = lax.axis_size("ka"), lax.axis_size("occ")
+    whole_square = pairs * holders == orbitals * orbitals
+    fits = momenta == 2 and orbitals == 2 and holders == 2 and rounds == 2
+    even = ring % 2 == 0 and ring > 4 and virtuals % BAND == 0 and auxiliary % LANES == 0
+    chosen = fused if whole_square and fits and even else general
+    return chosen(factors, occupied_energy, virtual_energy, conserve, pair_lists)
+
+
 def solution(mesh):
     in_specs = (
         P("ka", None, None, None, None),

time: 201 us -> 55.5 us (0.28)
  waiting for transfers between devices: 45 us -> 0 us
  Pallas kernels: 0 us -> 42.6 us
  loops' own time: 39.8 us -> 0 us
  matrix products: 39.1 us -> 0 us
  local copies, waits for them, and re-layouts: 45.3 us -> 12.6 us
  between operations: 21 us -> 0.07 us
  other arithmetic: 4.87 us -> 0 us
  starting transfers between devices: 4.36 us -> 0 us
    pallas_call x0 -> x1, Pallas kernels: none -> 42.6 us  [fused(): pl.pallas_call(functools.partial(fused_kernel, ring, virtuals, strips), o...]
    ppermute x4 -> x0, waiting for transfers between devices: 40.9 us -> none  [from_behind(): lax.ppermute(array, axis, [(i, (i + by) % size) for i in range(size)])]
    another operation x4 -> x0, loops' own time: 39.8 us -> none  [local(): lax.scan(add_pair, density[local_index], pair_lists[round_index])]
    dot_general x16 -> x0, matrix products: 39.1 us -> none  [the longest x8 20.2 us: density_term(): lax.dot_general(combined, stacked, (((1,), (1,)), ((), ())), preferred_el...]
    squeeze x6 -> x0, local copies, waits for them, and re-layouts: 11.2 us -> none  [the longest x2 5.41 us: local(): own_block = own[local_index]]
    dynamic_slice x19 -> x0, local copies, waits for them, and re-layouts: 8.37 us -> none  [the longest x8 5.05 us: pair_term(): occupied_sum = occupied_energy[leading] + occupied_energy[trailing]]
    slice x11 -> x0, local copies, waits for them, and re-layouts: 8.22 us -> none  [the longest x8 4.89 us: pair_term(): trailing = pair_row[1]]
    reshape x3 -> x1, local copies, waits for them, and re-layouts: 11.3 us -> 4.81 us  [fused(): raw = factors.reshape(momenta, orbitals, virtuals, parts, strips, LANES)]
  transfers between devices with their start and end apart: 7 -> 0, of which waited for: 4 -> 0; matrix products, arithmetic and copies ran while one was open for 22% -> 0% of each run, Pallas kernels for 0% -> 0%
where the time goes in v1:
time: 55.5 us; the launch traced here: 55.3 us
  Pallas kernels  42.6 us (77%)
  local copies, waits for them, and re-layouts  12.6 us (23%)
    pallas_call x1, Pallas kernels, fused(): pl.pallas_call(functools.partial(fused_kernel, ring, virtuals, strips), o...  42.6 us
    reshape x1, local copies, waits for them, and re-layouts, fused(): raw = factors.reshape(momenta, orbitals, virtuals, parts, strips, LANES)  4.81 us
    unnamed x8, local copies, waits for them, and re-layouts  4.15 us
    transpose x1, local copies, waits for them, and re-layouts, fused(): raw.transpose(0, 1, 2, 4, 3, 5).reshape(momenta, orbitals, raw_rows, LANES)  3.64 us

profile of v1, /device:TPU:0, one launch (start us, length us, event | category | flops | bytes accessed | tf_op | source)
XLA Modules:
  0.0 55.3 jit_solution(16827881680297791578)
XLA Ops:
  0.0 3.4 %copy.6 = bf16[2,2,192,2,768]{4,2,3,1,0:T(8,128)(2,1)} copy(bf16[2,2,192,2,768]{4,3,2,1,0:T(2,128)(2,1)} %param.5) | data formatting | bytes 4718592 | tf_op args[0]
  3.4 4.8 %reshape.6 = bf16[2,2,192,2,6,128]{5,4,2,3,1,0:T(8,128)(2,1)S(1)} reshape(bf16[2,2,192,2,768]{4,2,3,1,0:T(8,128)(2,1)} %copy.6) | data formatting | bytes 4718592 | tf_op jit(solution)/shard_map/reshape | solution.py:308
  8.2 0.0 copy-start
  8.2 0.0 copy-start.1
  8.2 0.0 copy-start.2
  8.2 3.6 %copy.7 = bf16[2,2,192,6,2,128]{5,4,3,2,1,0:T(2,128)(2,1)S(1)} copy(bf16[2,2,192,6,2,128]{5,3,2,4,1,0:T(8,128)(2,1)S(1)} %bitcast.7) | data formatting | bytes 4718592 | tf_op jit(solution)/shard_map/transpose | solution.py:309
  11.9 0.0 copy-done
  11.9 0.0 copy-done.1
  11.9 0.0 copy-done.2
  11.9 42.6 %density.1 = f32[2,96,2,192]{3,2,1,0:T(2,128)S(1)} custom-call(s32[2,2]{1,0:T(2,128)S(1)} %copy-done, f32[2]{0:T(128)S(1)} %copy-done.2, bf16[2,192]{1,0:T(2,128)(2,1)S(1)} %copy-done.1, bf16[2,2,2304,128]{3,2,1,0:T(8,128)(2,1)S(1)} %bitcast.6), custom_call_target="tpu_custom_call" | custom-call | tf_op jit(solution)/shard_map/density/pallas_call | solution.py:312
  54.5 0.7 %copy.9 = f32[2,96,2,192]{3,2,1,0:T(2,128)} copy(f32[2,96,2,192]{3,2,1,0:T(2,128)S(1)} %density.1) | data formatting | bytes 589824
Async XLA Ops:
  8.2 3.7 %copy-start = (s32[2,2]{1,0:T(2,128)S(1)}, s32[2,2]{1,0:T(2,128)}, u32[]{:S(2)}) copy-start(s32[2,2]{1,0:T(2,128)} %conserve_ref.1) | copy-start | bytes 52
  8.2 3.7 %copy-start.1 = (bf16[2,192]{1,0:T(2,128)(2,1)S(1)}, bf16[2,192]{1,0:T(2,128)(2,1)}, u32[]{:S(2)}) copy-start(bf16[2,192]{1,0:T(2,128)(2,1)} %energy_ref.1) | copy-start | bytes 2308
  8.2 3.7 %copy-start.2 = (f32[2]{0:T(128)S(1)}, f32[2]{0:T(128)}, u32[]{:S(2)}) copy-start(f32[2]{0:T(128)} %occupied_ref.1) | copy-start | bytes 28

commit v2 on v1

--- a/solution.py
+++ b/solution.py
@@ -9,7 +9,8 @@
 
 LANES = 128
 BAND = 64
-PIECE = 16
+STEP = 16
+PIECE = 8
 
 
 def from_behind(array, axis, by):
@@ -93,9 +94,9 @@
 
 
 def fused_kernel(
-    ring, virtuals, strips,
+    ring, virtuals, auxiliary,
     conserve_ref, occupied_ref, energy_ref, factors_ref, out_ref,
-    own_raw, mate_raw, wide, own, mate, energy_in, energy_left, energy_rows, products, total, incoming,
+    own_raw, mate_raw, own, mate, energy_in, energy_left, energy_rows, products, total, incoming,
     own_sem, far_send, far_recv, near_send, near_recv,
     energy_send, energy_recv, swap_send, swap_recv,
 ):
@@ -104,42 +105,50 @@
     core = lax.axis_index("occ")
     other = 1 - core
     odd = lax.rem(me, 2)
-    span = 2 * strips
     half = virtuals // 2
     pieces = virtuals // PIECE
+    steps = virtuals // STEP
     bands = virtuals // BAND
-    subs = BAND // PIECE
+    per_step = STEP // PIECE
+    per_band = BAND // STEP
 
     def at(step):
         return lax.rem(me + step + ring, ring)
 
     near = at(1 - 2 * odd)
 
-    own_copy = pltpu.make_async_copy(factors_ref, own_raw, own_sem)
-    own_copy.start()
+    def own_copy(momentum, index):
+        return pltpu.make_async_copy(
+            factors_ref.at[momentum], own_raw.at[momentum], own_sem.at[index]
+        )
+
+    own_copy(core, 0).start()
+    own_copy(other, 1).start()
 
     barrier = pltpu.get_barrier_semaphore()
     for step in (1, 2, -1, -2):
         pl.semaphore_signal(barrier, inc=1, device_id=(at(step), core), device_id_type=mesh_id)
     pl.semaphore_signal(barrier, inc=1, device_id=(me, other), device_id_type=mesh_id)
-    pl.semaphore_wait(barrier, 5)
-
-    def rows_of(piece):
-        return pl.ds(pl.multiple_of(piece * (PIECE * span), PIECE * span), PIECE * span)
+
+    def piece_rows(piece):
+        return pl.ds(pl.multiple_of(piece * PIECE, PIECE), PIECE)
+
+    def step_rows(step):
+        return pl.ds(pl.multiple_of(step * STEP, STEP), STEP)
 
     def far_copy(piece):
         return pltpu.make_async_remote_copy(
-            src_ref=factors_ref.at[core, :, rows_of(piece), :],
-            dst_ref=mate_raw.at[1, :, rows_of(piece), :],
+            src_ref=own_raw.at[core, :, piece_rows(piece)],
+            dst_ref=mate_raw.at[1, :, piece_rows(piece)],
             send_sem=far_send.at[piece], recv_sem=far_recv.at[piece],
             device_id=(at(2), core), device_id_type=mesh_id,
         )
 
     def near_copy(piece, relay):
-        source = mate_raw.at[1] if relay else factors_ref.at[core]
+        source = mate_raw.at[1] if relay else own_raw.at[core]
         return pltpu.make_async_remote_copy(
-            src_ref=source.at[:, rows_of(piece), :],
-            dst_ref=mate_raw.at[0, :, rows_of(piece), :],
+            src_ref=source.at[:, piece_rows(piece)],
+            dst_ref=mate_raw.at[0, :, piece_rows(piece)],
             send_sem=near_send.at[piece], recv_sem=near_recv.at[piece],
             device_id=(near, core), device_id_type=mesh_id,
         )
@@ -151,8 +160,8 @@
             device_id=(at(slot + 1), core), device_id_type=mesh_id,
         )
 
-    energy_copy(0).start()
-    energy_copy(1).start()
+    own_copy(core, 0).wait()
+    pl.semaphore_wait(barrier, 5)
 
     def send_piece(piece, carry):
         far_copy(piece).start()
@@ -163,70 +172,74 @@
 
         return carry
 
-    lax.fori_loop(0, pieces, send_piece, 0)
+    lax.fori_loop(0, 2, send_piece, 0)
+    energy_copy(0).start()
+    energy_copy(1).start()
+    lax.fori_loop(2, pieces, send_piece, 0)
 
     chosen = []
     for slot in range(2):
         mirror = lax.rem(2 - lax.rem(conserve_ref[0, slot], 2), 2)
         chosen.append(jnp.where(mirror == core, 0, 1))
 
-    total[...] = jnp.zeros_like(total)
-    own_copy.wait()
+    own_copy(other, 1).wait()
+
+    def forward(piece):
+        far_copy(piece).wait_recv()
+
+        @pl.when(odd == 1)
+        def _():
+            near_copy(piece, True).start()
 
     def shape_own(step, carry):
-        momentum_orbital = step // pieces
-        piece = lax.rem(step, pieces)
-        momentum = momentum_orbital // 2
-        orbital = lax.rem(momentum_orbital, 2)
-        wide[...] = own_raw[momentum, orbital, rows_of(piece), :].astype(jnp.float32)
-        row = pl.ds(pl.multiple_of(orbital * virtuals + piece * PIECE, PIECE), PIECE)
-        for column in range(span):
-            block = wide[pl.ds(column, PIECE, stride=span), :].astype(jnp.bfloat16)
-            own[momentum, row, pl.ds(column * LANES, LANES)] = block
+        for momentum in range(2):
+            for orbital in range(2):
+                row = pl.ds(pl.multiple_of(orbital * virtuals + step * STEP, STEP), STEP)
+                for part in range(2):
+                    own[momentum, row, pl.ds(part * auxiliary, auxiliary)] = own_raw[
+                        momentum, orbital, step_rows(step), part, :
+                    ]
         return carry
 
-    lax.fori_loop(0, 4 * pieces, shape_own, 0)
-
-    diagonal = lax.broadcasted_iota(jnp.int32, (virtuals, virtuals), 0) == lax.broadcasted_iota(
-        jnp.int32, (virtuals, virtuals), 1
-    )
-    mine = energy_ref[...].astype(jnp.float32)
-    for momentum in range(2):
-        spread = jnp.where(diagonal, mine[momentum : momentum + 1, :], 0.0)
-        column = jnp.sum(spread, axis=1, keepdims=True)
-        energy_left[momentum] = jnp.broadcast_to(column, (virtuals, LANES))
-    for slot in range(2):
-        energy_copy(slot).wait()
-        theirs = energy_in[slot].astype(jnp.float32)
-        theirs = jnp.where(core == 0, theirs[0:1, :], theirs[1:2, :])
-        for band in range(bands):
-            part = theirs[:, band * BAND : (band + 1) * BAND]
-            energy_rows[slot, band] = jnp.broadcast_to(
-                jnp.concatenate([part, part], axis=1), (8, LANES)
-            )
+    def shape_mate(slot, step):
+        band = step // per_band
+        for orbital in range(2):
+            real = mate_raw[slot, orbital, step_rows(step), 0, :]
+            imaginary = mate_raw[slot, orbital, step_rows(step), 1, :]
+            first = orbital * 2 * BAND + lax.rem(step, per_band) * STEP
+            plain = pl.ds(pl.multiple_of(first, STEP), STEP)
+            turned = pl.ds(pl.multiple_of(first + BAND, STEP), STEP)
+            mate[slot, band, plain, pl.ds(0, auxiliary)] = real
+            mate[slot, band, plain, pl.ds(auxiliary, auxiliary)] = imaginary
+            mate[slot, band, turned, pl.ds(0, auxiliary)] = -imaginary
+            mate[slot, band, turned, pl.ds(auxiliary, auxiliary)] = real
+
+    def shape_energies():
+        diagonal = lax.broadcasted_iota(
+            jnp.int32, (virtuals, virtuals), 0
+        ) == lax.broadcasted_iota(jnp.int32, (virtuals, virtuals), 1)
+        mine = energy_ref[...].astype(jnp.float32)
+        for momentum in range(2):
+            spread = jnp.where(diagonal, mine[momentum : momentum + 1, :], 0.0)
+            column = jnp.sum(spread, axis=1, keepdims=True)
+            energy_left[momentum] = jnp.broadcast_to(column, (virtuals, LANES))
+        for slot in range(2):
+            energy_copy(slot).wait()
+            theirs = energy_in[slot].astype(jnp.float32)
+            theirs = jnp.where(core == 0, theirs[0:1, :], theirs[1:2, :])
+            for band in range(bands):
+                part = theirs[:, band * BAND : (band + 1) * BAND]
+                energy_rows[slot, band] = jnp.broadcast_to(
+                    jnp.concatenate([part, part], axis=1), (8, LANES)
+                )
 
     sign = jnp.where(lax.broadcasted_iota(jnp.int32, (virtuals, LANES), 1) < BAND, -1.0, 1.0)
 
-    def shape_mate(slot, piece, sub):
-        for orbital in range(2):
-            wide[...] = mate_raw[slot, orbital, rows_of(piece), :].astype(jnp.float32)
-            first = orbital * 2 * BAND + sub * PIECE
-            plain = pl.ds(pl.multiple_of(first, PIECE), PIECE)
-            turned = pl.ds(pl.multiple_of(first + BAND, PIECE), PIECE)
-            for strip in range(strips):
-                real = wide[pl.ds(2 * strip, PIECE, stride=span), :]
-                imaginary = wide[pl.ds(2 * strip + 1, PIECE, stride=span), :]
-                left = pl.ds(2 * strip * LANES, LANES)
-                right = pl.ds((2 * strip + 1) * LANES, LANES)
-                mate[slot, plain, left] = real.astype(jnp.bfloat16)
-                mate[slot, plain, right] = imaginary.astype(jnp.bfloat16)
-                mate[slot, turned, left] = (-imaginary).astype(jnp.bfloat16)
-                mate[slot, turned, right] = real.astype(jnp.bfloat16)
-
     def add_band(slot, band):
-        momentum = chosen[slot]
+        momentum = jnp.where(slot == 1, chosen[1], chosen[0])
         products[...] = lax.dot_general(
-            own[momentum], mate[slot], (((1,), (1,)), ((), ())), preferred_element_type=jnp.float32
+            own[momentum], mate[slot, band], (((1,), (1,)), ((), ())),
+            preferred_element_type=jnp.float32,
         )
         base = energy_left[momentum] + energy_rows[slot, band][0:1, :]
         amplitudes = {}
@@ -250,26 +263,35 @@
             left, right, (((1,), (1,)), ((), ())), preferred_element_type=jnp.float32
         )
 
-    def band_step(band, carry):
-        def piece_step(sub, inner):
-            piece = band * subs + sub
-            far_copy(piece).wait_recv()
-
-            @pl.when(odd == 1)
-            def _():
-                near_copy(piece, True).start()
-
-            shape_mate(1, piece, sub)
-            near_copy(piece, False).wait_recv()
-            shape_mate(0, piece, sub)
-            return inner
-
-        lax.fori_loop(0, subs, piece_step, 0)
-        add_band(1, band)
-        add_band(0, band)
+    def far_step(step):
+        for piece in range(per_step):
+            forward(step * per_step + piece)
+        shape_mate(1, step)
+
+    def near_step(step):
+        for piece in range(per_step):
+            near_copy(step * per_step + piece, False).wait_recv()
+        shape_mate(0, step)
+
+    total[...] = jnp.zeros_like(total)
+    lax.fori_loop(0, steps // 2, shape_own, 0)
+    far_step(0)
+    lax.fori_loop(steps // 2, steps, shape_own, 0)
+    shape_energies()
+
+    def main_step(step, carry):
+        far_step(step)
+        near_step(step - 1)
+        phase = lax.rem(step, per_band)
+        ready = jnp.logical_and(step >= per_band, jnp.logical_or(phase == 1, phase == 2))
+
+        @pl.when(ready)
+        def _():
+            add_band(2 - phase, step // per_band - 1)
+
         return carry
 
-    lax.fori_loop(0, bands, band_step, 0)
+    lax.fori_loop(1, steps, main_step, 0)
 
     def swap_copy(slot):
         return pltpu.make_async_remote_copy(
@@ -279,8 +301,18 @@
             device_id=(me, other), device_id_type=mesh_id,
         )
 
-    for slot in (1, 0):
-        swap_copy(slot).start()
+    add_band(1, bands - 1)
+    swap_copy(1).start()
+    near_step(steps - 1)
+    add_band(0, bands - 1)
+    swap_copy(0).start()
+
+    def drain(piece, carry):
+        far_copy(piece).wait_send()
+        near_copy(piece, False).wait_send()
+        return carry
+
+    lax.fori_loop(0, pieces, drain, 0)
     for slot in (1, 0):
         swap_copy(slot).wait()
 
@@ -292,25 +324,15 @@
         for part in range(2):
             out_ref[momentum, :, part, :] = value[:, part * virtuals : (part + 1) * virtuals]
 
-    def drain(piece, carry):
-        far_copy(piece).wait_send()
-        near_copy(piece, False).wait_send()
-        return carry
-
-    lax.fori_loop(0, pieces, drain, 0)
-
 
 def fused(factors, occupied_energy, virtual_energy, conserve, pair_lists):
     momenta, orbitals, virtuals, parts, auxiliary = factors.shape
-    strips = auxiliary // LANES
     ring = lax.axis_size("ka")
-    raw_rows = virtuals * parts * strips
-    raw = factors.reshape(momenta, orbitals, virtuals, parts, strips, LANES)
-    raw = raw.transpose(0, 1, 2, 4, 3, 5).reshape(momenta, orbitals, raw_rows, LANES)
     pieces = virtuals // PIECE
+    bands = virtuals // BAND
     dma = pltpu.SemaphoreType.DMA
     return pl.pallas_call(
-        functools.partial(fused_kernel, ring, virtuals, strips),
+        functools.partial(fused_kernel, ring, virtuals, auxiliary),
         out_shape=jax.ShapeDtypeStruct((momenta, virtuals // 2, 2, virtuals), jnp.float32),
         in_specs=[
             pl.BlockSpec(memory_space=pltpu.SMEM),
@@ -320,26 +342,25 @@
         ],
         out_specs=pl.BlockSpec(memory_space=pltpu.VMEM),
         scratch_shapes=[
-            pltpu.VMEM((momenta, orbitals, raw_rows, LANES), jnp.bfloat16),
-            pltpu.VMEM((2, orbitals, raw_rows, LANES), jnp.bfloat16),
-            pltpu.VMEM((PIECE * parts * strips, LANES), jnp.float32),
+            pltpu.VMEM((momenta, orbitals, virtuals, parts, auxiliary), jnp.bfloat16),
+            pltpu.VMEM((2, orbitals, virtuals, parts, auxiliary), jnp.bfloat16),
             pltpu.VMEM((momenta, orbitals * virtuals, parts * auxiliary), jnp.bfloat16),
-            pltpu.VMEM((2, orbitals * 2 * BAND, parts * auxiliary), jnp.bfloat16),
+            pltpu.VMEM((2, bands, orbitals * 2 * BAND, parts * auxiliary), jnp.bfloat16),
             pltpu.VMEM((2, momenta, virtuals), jnp.bfloat16),
             pltpu.VMEM((momenta, virtuals, LANES), jnp.float32),
-            pltpu.VMEM((2, virtuals // BAND, 8, LANES), jnp.float32),
+            pltpu.VMEM((2, bands, 8, LANES), jnp.float32),
             pltpu.VMEM((orbitals * virtuals, orbitals * 2 * BAND), jnp.float32),
             pltpu.VMEM((2, virtuals, 2 * virtuals), jnp.float32),
             pltpu.VMEM((2, virtuals // 2, 2 * virtuals), jnp.float32),
-            dma,
+            dma((2,)),
             dma((pieces,)), dma((pieces,)), dma((pieces,)), dma((pieces,)),
             dma((2,)), dma((2,)), dma((2,)), dma((2,)),
         ],
         compiler_params=pltpu.CompilerParams(
-            collective_id=0, has_side_effects=True, vmem_limit_bytes=48 * 1024 * 1024
+            collective_id=0, has_side_effects=True, vmem_limit_bytes=56 * 1024 * 1024
         ),
         name="density",
-    )(conserve, occupied_energy, virtual_energy, raw)
+    )(conserve, occupied_energy, virtual_energy, factors)
 
 
 def local(factors, occupied_energy, virtual_energy, conserve, pair_lists):

time: 55.5 us -> 45.4 us (0.82)
  local copies, waits for them, and re-layouts: 12.6 us -> 1.88 us
  Pallas kernels: 42.6 us -> 43.3 us
    reshape x1 -> x0, local copies, waits for them, and re-layouts: 4.81 us -> none  [fused(): raw = factors.reshape(momenta, orbitals, virtuals, parts, strips, LANES)]
    transpose x1 -> x0, local copies, waits for them, and re-layouts: 3.64 us -> none  [fused(): raw.transpose(0, 1, 2, 4, 3, 5).reshape(momenta, orbitals, raw_rows, LANES)]
    unnamed x8 -> x1, local copies, waits for them, and re-layouts: 4.15 us -> 1.88 us
    pallas_call x1, Pallas kernels: 42.6 us -> 43.3 us  [fused(): pl.pallas_call(functools.partial(fused_kernel, ring, virtuals, auxiliary)...]
where the time goes in v2:
time: 45.4 us; the launch traced here: 45.2 us
  Pallas kernels  43.3 us (95%)
  local copies, waits for them, and re-layouts  1.88 us (4%)
    pallas_call x1, Pallas kernels, fused(): pl.pallas_call(functools.partial(fused_kernel, ring, virtuals, auxiliary)...  43.3 us
    unnamed x1, local copies, waits for them, and re-layouts  1.88 us

profile of v2, /device:TPU:0, one launch (start us, length us, event | category | flops | bytes accessed | tf_op | source)
XLA Modules:
  0.0 45.2 jit_solution(2362677757242771702)
XLA Ops:
  0.0 43.3 %density.1 = f32[2,96,2,192]{3,2,1,0:T(2,128)} custom-call(s32[2,2]{1,0:T(2,128)} %conserve_ref.1, f32[2]{0:T(128)} %occupied_ref.1, bf16[2,192]{1,0:T(2,128)(2,1)} %energy_ref.1, bf16[2,2,192,2,768]{4,3,2,1,0:T(2,128)(2,1)} %factors_ref.1), custom_call_target="tpu_custom_call" | custom-call | tf_op jit(solution)/shard_map/density/pallas_call | solution.py:334
  43.3 1.9 %copy.6 = f32[2,96,2,192]{3,2,1,0:T(2,128)} copy(f32[2,96,2,192]{3,2,1,0:T(2,128)} %density.1) | data formatting | bytes 589824

commit v3 on v2

--- a/solution.py
+++ b/solution.py
@@ -95,9 +95,9 @@
 
 def fused_kernel(
     ring, virtuals, auxiliary,
-    conserve_ref, occupied_ref, energy_ref, factors_ref, out_ref,
-    own_raw, mate_raw, own, mate, energy_in, energy_left, energy_rows, products, total, incoming,
-    own_sem, far_send, far_recv, near_send, near_recv,
+    conserve_hbm, occupied_hbm, energy_hbm, factors_ref, out_ref,
+    conserve_ref, occupied_ref, energy_ref, own_raw, mate_raw, own, mate, energy_in, energy_left, energy_rows, products, total, incoming,
+    small_sem, own_sem, far_send, far_recv, near_send, near_recv,
     energy_send, energy_recv, swap_send, swap_recv,
 ):
     mesh_id = pl.DeviceIdType.MESH
@@ -122,13 +122,20 @@
             factors_ref.at[momentum], own_raw.at[momentum], own_sem.at[index]
         )
 
+    def small_copies():
+        return (
+            pltpu.make_async_copy(conserve_hbm, conserve_ref, small_sem.at[0]),
+            pltpu.make_async_copy(occupied_hbm, occupied_ref, small_sem.at[1]),
+            pltpu.make_async_copy(energy_hbm, energy_ref, small_sem.at[2]),
+        )
+
+    barrier = pltpu.get_barrier_semaphore()
+    for place in ((at(-2), core), (near, core), (me, other)):
+        pl.semaphore_signal(barrier, inc=1, device_id=place, device_id_type=mesh_id)
     own_copy(core, 0).start()
+    for copy in small_copies():
+        copy.start()
     own_copy(other, 1).start()
-
-    barrier = pltpu.get_barrier_semaphore()
-    for step in (1, 2, -1, -2):
-        pl.semaphore_signal(barrier, inc=1, device_id=(at(step), core), device_id_type=mesh_id)
-    pl.semaphore_signal(barrier, inc=1, device_id=(me, other), device_id_type=mesh_id)
 
     def piece_rows(piece):
         return pl.ds(pl.multiple_of(piece * PIECE, PIECE), PIECE)
@@ -153,15 +160,22 @@
             device_id=(near, core), device_id_type=mesh_id,
         )
 
-    def energy_copy(slot):
+    def energy_far():
         return pltpu.make_async_remote_copy(
-            src_ref=energy_ref, dst_ref=energy_in.at[slot],
-            send_sem=energy_send.at[slot], recv_sem=energy_recv.at[slot],
-            device_id=(at(slot + 1), core), device_id_type=mesh_id,
+            src_ref=energy_ref, dst_ref=energy_in.at[1],
+            send_sem=energy_send.at[1], recv_sem=energy_recv.at[1],
+            device_id=(at(2), core), device_id_type=mesh_id,
+        )
+
+    def energy_near(relay):
+        return pltpu.make_async_remote_copy(
+            src_ref=energy_in.at[1] if relay else energy_ref, dst_ref=energy_in.at[0],
+            send_sem=energy_send.at[0], recv_sem=energy_recv.at[0],
+            device_id=(near, core), device_id_type=mesh_id,
         )
 
     own_copy(core, 0).wait()
-    pl.semaphore_wait(barrier, 5)
+    pl.semaphore_wait(barrier, 3)
 
     def send_piece(piece, carry):
         far_copy(piece).start()
@@ -173,8 +187,14 @@
         return carry
 
     lax.fori_loop(0, 2, send_piece, 0)
-    energy_copy(0).start()
-    energy_copy(1).start()
+    for copy in small_copies():
+        copy.wait()
+    energy_far().start()
+
+    @pl.when(odd == 0)
+    def _():
+        energy_near(False).start()
+
     lax.fori_loop(2, pieces, send_piece, 0)
 
     chosen = []
@@ -223,8 +243,8 @@
             spread = jnp.where(diagonal, mine[momentum : momentum + 1, :], 0.0)
             column = jnp.sum(spread, axis=1, keepdims=True)
             energy_left[momentum] = jnp.broadcast_to(column, (virtuals, LANES))
+        energy_near(False).wait_recv()
         for slot in range(2):
-            energy_copy(slot).wait()
             theirs = energy_in[slot].astype(jnp.float32)
             theirs = jnp.where(core == 0, theirs[0:1, :], theirs[1:2, :])
             for band in range(bands):
@@ -276,11 +296,21 @@
     total[...] = jnp.zeros_like(total)
     lax.fori_loop(0, steps // 2, shape_own, 0)
     far_step(0)
+    energy_far().wait_recv()
+
+    @pl.when(odd == 1)
+    def _():
+        energy_near(True).start()
+
     lax.fori_loop(steps // 2, steps, shape_own, 0)
+    far_step(1)
     shape_energies()
 
     def main_step(step, carry):
-        far_step(step)
+        @pl.when(step > 1)
+        def _():
+            far_step(step)
+
         near_step(step - 1)
         phase = lax.rem(step, per_band)
         ready = jnp.logical_and(step >= per_band, jnp.logical_or(phase == 1, phase == 2))
@@ -313,6 +343,8 @@
         return carry
 
     lax.fori_loop(0, pieces, drain, 0)
+    energy_far().wait_send()
+    energy_near(False).wait_send()
     for slot in (1, 0):
         swap_copy(slot).wait()
 
@@ -335,13 +367,16 @@
         functools.partial(fused_kernel, ring, virtuals, auxiliary),
         out_shape=jax.ShapeDtypeStruct((momenta, virtuals // 2, 2, virtuals), jnp.float32),
         in_specs=[
-            pl.BlockSpec(memory_space=pltpu.SMEM),
-            pl.BlockSpec(memory_space=pltpu.SMEM),
-            pl.BlockSpec(memory_space=pltpu.VMEM),
-            pl.BlockSpec(memory_space=pl.ANY),
+            pl.BlockSpec(memory_space=pltpu.HBM),
+            pl.BlockSpec(memory_space=pltpu.HBM),
+            pl.BlockSpec(memory_space=pltpu.HBM),
+            pl.BlockSpec(memory_space=pltpu.HBM),
         ],
         out_specs=pl.BlockSpec(memory_space=pltpu.VMEM),
         scratch_shapes=[
+            pltpu.SMEM(conserve.shape, conserve.dtype),
+            pltpu.SMEM(occupied_energy.shape, occupied_energy.dtype),
+            pltpu.VMEM(virtual_energy.shape, virtual_energy.dtype),
             pltpu.VMEM((momenta, orbitals, virtuals, parts, auxiliary), jnp.bfloat16),
             pltpu.VMEM((2, orbitals, virtuals, parts, auxiliary), jnp.bfloat16),
             pltpu.VMEM((momenta, orbitals * virtuals, parts * auxiliary), jnp.bfloat16),
@@ -352,12 +387,12 @@
             pltpu.VMEM((orbitals * virtuals, orbitals * 2 * BAND), jnp.float32),
             pltpu.VMEM((2, virtuals, 2 * virtuals), jnp.float32),
             pltpu.VMEM((2, virtuals // 2, 2 * virtuals), jnp.float32),
-            dma((2,)),
+            dma((3,)), dma((2,)),
             dma((pieces,)), dma((pieces,)), dma((pieces,)), dma((pieces,)),
             dma((2,)), dma((2,)), dma((2,)), dma((2,)),
         ],
         compiler_params=pltpu.CompilerParams(
-            collective_id=0, has_side_effects=True, vmem_limit_bytes=56 * 1024 * 1024
+            collective_id=0, has_side_effects=True, vmem_limit_bytes=22 * 1024 * 1024
         ),
         name="density",
     )(conserve, occupied_energy, virtual_energy, factors)

time: 45.4 us -> 45.5 us (level)
  local copies, waits for them, and re-layouts: 1.88 us -> 4.42 us
  Pallas kernels: 43.3 us -> 40.9 us
    unnamed x1 -> x9, local copies, waits for them, and re-layouts: 1.88 us -> 4.42 us
    pallas_call x1, Pallas kernels: 43.3 us -> 40.9 us  [fused(): pl.pallas_call(functools.partial(fused_kernel, ring, virtuals, auxiliary)...]
where the time goes in v3:
time: 45.5 us; the launch traced here: 45.3 us
  Pallas kernels  40.9 us (90%)
  local copies, waits for them, and re-layouts  4.42 us (10%)
    pallas_call x1, Pallas kernels, fused(): pl.pallas_call(functools.partial(fused_kernel, ring, virtuals, auxiliary)...  40.9 us
    unnamed x9, local copies, waits for them, and re-layouts  4.42 us

profile of v3, /device:TPU:0, one launch (start us, length us, event | category | flops | bytes accessed | tf_op | source)
XLA Modules:
  0.0 45.3 jit_solution(1377430990930795976)
XLA Ops:
  0.0 0.0 copy-start
  0.0 1.7 %copy-done = bf16[2,2,192,2,768]{4,3,2,1,0:T(2,128)(2,1)S(1)} copy-done((bf16[2,2,192,2,768]{4,3,2,1,0:T(2,128)(2,1)S(1)}, bf16[2,2,192,2,768]{4,3,2,1,0:T(2,128)(2,1)}, u32[]{:S(2)}) %copy-start) | copy-done | bytes 2359320
  1.7 0.0 copy-start.1
  1.7 0.7 %copy-done.1 = s32[2,2]{1,0:T(2,128)S(1)} copy-done((s32[2,2]{1,0:T(2,128)S(1)}, s32[2,2]{1,0:T(2,128)}, u32[]{:S(2)}) %copy-start.1) | copy-done | bytes 40
  2.3 0.0 copy-start.2
  2.3 0.7 %copy-done.2 = bf16[2,192]{1,0:T(2,128)(2,1)S(1)} copy-done((bf16[2,192]{1,0:T(2,128)(2,1)S(1)}, bf16[2,192]{1,0:T(2,128)(2,1)}, u32[]{:S(2)}) %copy-start.2) | copy-done | bytes 792
  3.0 0.0 copy-start.3
  3.0 0.7 %copy-done.3 = f32[2]{0:T(128)S(1)} copy-done((f32[2]{0:T(128)S(1)}, f32[2]{0:T(128)}, u32[]{:S(2)}) %copy-start.3) | copy-done | bytes 32
  3.7 40.9 %density.1 = f32[2,96,2,192]{3,2,1,0:T(2,128)S(1)} custom-call(s32[2,2]{1,0:T(2,128)S(1)} %copy-done.1, f32[2]{0:T(128)S(1)} %copy-done.3, bf16[2,192]{1,0:T(2,128)(2,1)S(1)} %copy-done.2, bf16[2,2,192,2,768]{4,3,2,1,0:T(2,128)(2,1)S(1)} %copy-done), custom_call_target="tpu_custom_call" | custom-call | tf_op jit(solution)/shard_map/density/pallas_call | solution.py:366
  44.6 0.7 %copy.6 = f32[2,96,2,192]{3,2,1,0:T(2,128)} copy(f32[2,96,2,192]{3,2,1,0:T(2,128)S(1)} %density.1) | data formatting | bytes 589824
Async XLA Ops:
  0.0 1.7 %copy-start = (bf16[2,2,192,2,768]{4,3,2,1,0:T(2,128)(2,1)S(1)}, bf16[2,2,192,2,768]{4,3,2,1,0:T(2,128)(2,1)}, u32[]{:S(2)}) copy-start(bf16[2,2,192,2,768]{4,3,2,1,0:T(2,128)(2,1)} %factors_ref.1) | copy-start | bytes 7077892
  1.7 0.7 %copy-start.1 = (s32[2,2]{1,0:T(2,128)S(1)}, s32[2,2]{1,0:T(2,128)}, u32[]{:S(2)}) copy-start(s32[2,2]{1,0:T(2,128)} %conserve_hbm.1) | copy-start | bytes 52
  2.3 0.7 %copy-start.2 = (bf16[2,192]{1,0:T(2,128)(2,1)S(1)}, bf16[2,192]{1,0:T(2,128)(2,1)}, u32[]{:S(2)}) copy-start(bf16[2,192]{1,0:T(2,128)(2,1)} %energy_hbm.1) | copy-start | bytes 2308
  3.0 0.7 %copy-start.3 = (f32[2]{0:T(128)S(1)}, f32[2]{0:T(128)}, u32[]{:S(2)}) copy-start(f32[2]{0:T(128)} %occupied_hbm.1) | copy-start | bytes 28

commit v4 on v3

--- a/solution.py
+++ b/solution.py
@@ -10,7 +10,7 @@
 LANES = 128
 BAND = 64
 STEP = 16
-PIECE = 8
+PIECE = 4
 
 
 def from_behind(array, axis, by):
@@ -96,7 +96,7 @@
 def fused_kernel(
     ring, virtuals, auxiliary,
     conserve_hbm, occupied_hbm, energy_hbm, factors_ref, out_ref,
-    conserve_ref, occupied_ref, energy_ref, own_raw, mate_raw, own, mate, energy_in, energy_left, energy_rows, products, total, incoming,
+    conserve_ref, occupied_ref, energy_ref, own_raw, mate_raw, own, mate, energy_in, energy_left, inverse, products, total, incoming, partial,
     small_sem, own_sem, far_send, far_recv, near_send, near_recv,
     energy_send, energy_recv, swap_send, swap_recv,
 ):
@@ -235,6 +235,8 @@
             mate[slot, band, turned, pl.ds(auxiliary, auxiliary)] = real
 
     def shape_energies():
+        sums = [occupied_ref[0] + occupied_ref[0], occupied_ref[0] + occupied_ref[1]]
+        sums.append(occupied_ref[1] + occupied_ref[1])
         diagonal = lax.broadcasted_iota(
             jnp.int32, (virtuals, virtuals), 0
         ) == lax.broadcasted_iota(jnp.int32, (virtuals, virtuals), 1)
@@ -249,9 +251,10 @@
             theirs = jnp.where(core == 0, theirs[0:1, :], theirs[1:2, :])
             for band in range(bands):
                 part = theirs[:, band * BAND : (band + 1) * BAND]
-                energy_rows[slot, band] = jnp.broadcast_to(
-                    jnp.concatenate([part, part], axis=1), (8, LANES)
-                )
+                row = jnp.concatenate([part, part], axis=1)
+                base = energy_left[chosen[slot]] + row
+                for kind in range(3):
+                    inverse[slot, band, kind] = 1.0 / (base - sums[kind])
 
     sign = jnp.where(lax.broadcasted_iota(jnp.int32, (virtuals, LANES), 1) < BAND, -1.0, 1.0)
 
@@ -261,13 +264,11 @@
             own[momentum], mate[slot, band], (((1,), (1,)), ((), ())),
             preferred_element_type=jnp.float32,
         )
-        base = energy_left[momentum] + energy_rows[slot, band][0:1, :]
         amplitudes = {}
         for i in range(2):
             for j in range(2):
-                gap = base - (occupied_ref[i] + occupied_ref[j])
                 value = products[i * virtuals : (i + 1) * virtuals, j * LANES : (j + 1) * LANES]
-                amplitudes[i, j] = value / gap
+                amplitudes[i, j] = value * inverse[slot, band, i + j]
         combined, rounded, turned = [], [], []
         for i in range(2):
             for j in range(2):
@@ -345,14 +346,14 @@
     lax.fori_loop(0, pieces, drain, 0)
     energy_far().wait_send()
     energy_near(False).wait_send()
-    for slot in (1, 0):
-        swap_copy(slot).wait()
-
     here = pl.ds(pl.multiple_of(core * half, half), half)
+    swap_copy(1).wait()
     for momentum in range(2):
-        value = jnp.zeros((half, 2 * virtuals), jnp.float32)
-        for slot in (1, 0):
-            value += jnp.where(chosen[slot] == momentum, total[slot, here, :], incoming[slot])
+        known = jnp.where(chosen[1] == momentum, total[1, here, :], incoming[1])
+        partial[momentum] = known + jnp.where(chosen[0] == momentum, total[0, here, :], 0.0)
+    swap_copy(0).wait()
+    for momentum in range(2):
+        value = partial[momentum] + jnp.where(chosen[0] == momentum, 0.0, incoming[0])
         for part in range(2):
             out_ref[momentum, :, part, :] = value[:, part * virtuals : (part + 1) * virtuals]
 
@@ -383,16 +384,17 @@
             pltpu.VMEM((2, bands, orbitals * 2 * BAND, parts * auxiliary), jnp.bfloat16),
             pltpu.VMEM((2, momenta, virtuals), jnp.bfloat16),
             pltpu.VMEM((momenta, virtuals, LANES), jnp.float32),
-            pltpu.VMEM((2, bands, 8, LANES), jnp.float32),
+            pltpu.VMEM((2, bands, 3, virtuals, LANES), jnp.float32),
             pltpu.VMEM((orbitals * virtuals, orbitals * 2 * BAND), jnp.float32),
             pltpu.VMEM((2, virtuals, 2 * virtuals), jnp.float32),
+            pltpu.VMEM((2, virtuals // 2, 2 * virtuals), jnp.float32),
             pltpu.VMEM((2, virtuals // 2, 2 * virtuals), jnp.float32),
             dma((3,)), dma((2,)),
             dma((pieces,)), dma((pieces,)), dma((pieces,)), dma((pieces,)),
             dma((2,)), dma((2,)), dma((2,)), dma((2,)),
         ],
         compiler_params=pltpu.CompilerParams(
-            collective_id=0, has_side_effects=True, vmem_limit_bytes=22 * 1024 * 1024
+            collective_id=0, has_side_effects=True, vmem_limit_bytes=54 * 1024 * 1024
         ),
         name="density",
     )(conserve, occupied_energy, virtual_energy, factors)

time: 45.5 us -> 45.2 us (level)
  local copies, waits for them, and re-layouts: 4.42 us -> 1.88 us
  Pallas kernels: 40.9 us -> 43.1 us
    unnamed x9 -> x1, local copies, waits for them, and re-layouts: 4.42 us -> 1.88 us
    pallas_call x1, Pallas kernels: 40.9 us -> 43.1 us  [fused(): pl.pallas_call(functools.partial(fused_kernel, ring, virtuals, auxiliary)...]
where the time goes in v4:
time: 45.2 us; the launch traced here: 45 us
  Pallas kernels  43.1 us (95%)
  local copies, waits for them, and re-layouts  1.88 us (4%)
    pallas_call x1, Pallas kernels, fused(): pl.pallas_call(functools.partial(fused_kernel, ring, virtuals, auxiliary)...  43.1 us
    unnamed x1, local copies, waits for them, and re-layouts  1.88 us

profile of v4, /device:TPU:0, one launch (start us, length us, event | category | flops | bytes accessed | tf_op | source)
XLA Modules:
  0.0 45.0 jit_solution(15040607182102324391)
XLA Ops:
  0.0 43.1 %density.1 = f32[2,96,2,192]{3,2,1,0:T(2,128)} custom-call(s32[2,2]{1,0:T(2,128)} %conserve_hbm.1, f32[2]{0:T(128)} %occupied_hbm.1, bf16[2,192]{1,0:T(2,128)(2,1)} %energy_hbm.1, bf16[2,2,192,2,768]{4,3,2,1,0:T(2,128)(2,1)} %factors_ref.1), custom_call_target="tpu_custom_call" | custom-call | tf_op jit(solution)/shard_map/density/pallas_call | solution.py:367
  43.1 1.9 %copy.6 = f32[2,96,2,192]{3,2,1,0:T(2,128)} copy(f32[2,96,2,192]{3,2,1,0:T(2,128)} %density.1) | data formatting | bytes 589824

commit v5 on v4

--- a/solution.py
+++ b/solution.py
@@ -366,7 +366,7 @@
     dma = pltpu.SemaphoreType.DMA
     return pl.pallas_call(
         functools.partial(fused_kernel, ring, virtuals, auxiliary),
-        out_shape=jax.ShapeDtypeStruct((momenta, virtuals // 2, 2, virtuals), jnp.float32),
+        out_shape=pltpu.VMEM((momenta, virtuals // 2, 2, virtuals), jnp.float32),
         in_specs=[
             pl.BlockSpec(memory_space=pltpu.HBM),
             pl.BlockSpec(memory_space=pltpu.HBM),

time: 45.2 us -> 43.3 us (0.958)
  local copies, waits for them, and re-layouts: 1.88 us -> 0.75 us
  Pallas kernels: 43.1 us -> 42.4 us
    unnamed x1, local copies, waits for them, and re-layouts: 1.88 us -> 0.75 us
    pallas_call x1, Pallas kernels: 43.1 us -> 42.4 us  [fused(): pl.pallas_call(functools.partial(fused_kernel, ring, virtuals, auxiliary)...]
where the time goes in v5:
time: 43.3 us; the launch traced here: 43.1 us
  Pallas kernels  42.4 us (98%)
  local copies, waits for them, and re-layouts  0.75 us (2%)
    pallas_call x1, Pallas kernels, fused(): pl.pallas_call(functools.partial(fused_kernel, ring, virtuals, auxiliary)...  42.4 us

profile of v5, /device:TPU:0, one launch (start us, length us, event | category | flops | bytes accessed | tf_op | source)
XLA Modules:
  0.0 43.1 jit_solution(6096028175541112026)
XLA Ops:
  0.0 42.4 %density.1 = f32[2,96,2,192]{3,2,1,0:T(2,128)S(1)} custom-call(s32[2,2]{1,0:T(2,128)} %conserve_hbm.1, f32[2]{0:T(128)} %occupied_hbm.1, bf16[2,192]{1,0:T(2,128)(2,1)} %energy_hbm.1, bf16[2,2,192,2,768]{4,3,2,1,0:T(2,128)(2,1)} %factors_ref.1), custom_call_target="tpu_custom_call" | custom-call | tf_op jit(solution)/shard_map/density/pallas_call | solution.py:367
  42.4 0.7 %copy.6 = f32[2,96,2,192]{3,2,1,0:T(2,128)} copy(f32[2,96,2,192]{3,2,1,0:T(2,128)S(1)} %density.1) | data formatting | bytes 589824

commit v6 on v5

--- a/solution.py
+++ b/solution.py
@@ -10,7 +10,7 @@
 LANES = 128
 BAND = 64
 STEP = 16
-PIECE = 4
+PIECE = 8
 
 
 def from_behind(array, axis, by):

time: 43.3 us -> 42.5 us (0.982)
  Pallas kernels: 42.4 us -> 41.6 us
    pallas_call x1, Pallas kernels: 42.4 us -> 41.6 us  [fused(): pl.pallas_call(functools.partial(fused_kernel, ring, virtuals, auxiliary)...]
where the time goes in v6:
time: 42.5 us; the launch traced here: 42.3 us
  Pallas kernels  41.6 us (98%)
  local copies, waits for them, and re-layouts  0.75 us (2%)
    pallas_call x1, Pallas kernels, fused(): pl.pallas_call(functools.partial(fused_kernel, ring, virtuals, auxiliary)...  41.6 us

profile of v6, /device:TPU:0, one launch (start us, length us, event | category | flops | bytes accessed | tf_op | source)
XLA Modules:
  0.0 42.3 jit_solution(16124680420717331305)
XLA Ops:
  0.0 41.6 %density.1 = f32[2,96,2,192]{3,2,1,0:T(2,128)S(1)} custom-call(s32[2,2]{1,0:T(2,128)} %conserve_hbm.1, f32[2]{0:T(128)} %occupied_hbm.1, bf16[2,192]{1,0:T(2,128)(2,1)} %energy_hbm.1, bf16[2,2,192,2,768]{4,3,2,1,0:T(2,128)(2,1)} %factors_ref.1), custom_call_target="tpu_custom_call" | custom-call | tf_op jit(solution)/shard_map/density/pallas_call | solution.py:367
  41.6 0.7 %copy.6 = f32[2,96,2,192]{3,2,1,0:T(2,128)} copy(f32[2,96,2,192]{3,2,1,0:T(2,128)S(1)} %density.1) | data formatting | bytes 589824
